TPU v7x, 256 devices: a whole 4x4x8 slice. The times are simulated.
256 devices in a mesh: section: 4 (over y), dp: 16 (over z, core), expert: 4 (over x).
Axes of the slice: x: 4, y: 4, z: 8, core: 2. Of those that a mesh axis runs over, the one named last changes fastest.
Arguments:
- inputs: bfloat16 [4, 8192, 2048], P('section', ('dp', 'expert')), may hold values from -6 to 6
- in_cache: bfloat16 [4, 8192, 2048], P('section', ('dp', 'expert')), may hold values from -6 to 6
- out_cache: bfloat16 [4, 8192, 2048], P('section', ('dp', 'expert')), may hold values from -6 to 6
- w_up: bfloat16 [4, 2048, 57344], P('section', None, ('dp', 'expert')), may hold values from -0.125 to 0.125
- w_down: bfloat16 [4, 57344, 2048], P('section', ('dp', 'expert')), may hold values from -0.0625 to 0.0625
- routing: int32 [4, 8192, 2], P('section', ('dp', 'expert')), may hold values from 0 to 7, all different within a row; in each aligned block of 128 rows (0 to 127, 128 to 255, ..., all dimensions but the last counted through in order) at most 32 rows name the same one
- gate_table: int32 [4, 8192, 2], P('section', ('dp', 'expert')), may hold values from 1 to 16
- lengths: int32 [512], P(('dp', 'expert')), may hold values from 1 to 16
- sample_map: int32 [512], replicated, may hold values from 0 to 511, as said below
Outputs:
- next_input: bfloat16 [4, 8192, 2048], P('section', ('dp', 'expert'))
- new_out_cache: bfloat16 [4, 8192, 2048], P('section', ('dp', 'expert'))
Inputs may be any that keep to these rules, and one draw needn't show every extreme that they name: `sample_map`: A permutation. Every sample keeps its index along expert; the samples of one device go to exactly 8 replicas, exactly 1 to each. `routing`: A row names 2 different experts; in the rows of one device each expert is named exactly 32 times.
All inputs are finite; a program needn't handle non-finite values.
Results may differ from a plain program's by a relative error of at most 0.007.
Values may be sent and summed in bfloat16 or wider, within the bound.
No kernel may reach another device: no remote copies, remote signals or barrier semaphores. Data moves between devices by JAX's collectives and lax.ppermute only.
A program may use at most 128 MiB of HBM per device.

v0:
```python
import jax
import jax.numpy as jnp
from jax import lax
from jax.sharding import PartitionSpec as P

EXPERTS = 8
TOPK = 2
ROWS = 16
SAMP_DEV = 8


def from_behind(value, axis, by):
    peers = lax.axis_size(axis)
    pairs = [(i, i + by) for i in range(peers) if 0 <= i + by < peers]
    return lax.ppermute(value, axis, pairs)


def per_device(inputs, in_cache, out_cache, w_up, w_down, routing, gate_table, lengths, sample_map):
    tok_rows = inputs.shape[1]
    feature_width = inputs.shape[2]
    dp_count = lax.axis_size("dp")
    expert_count = lax.axis_size("expert")
    group_size = dp_count * expert_count
    slice_count = group_size // EXPERTS
    own_dp = lax.axis_index("dp")
    own_device = own_dp * expert_count + lax.axis_index("expert")
    cap_slots = max(1, SAMP_DEV // dp_count)
    sample_ids = jnp.arange(SAMP_DEV, dtype=jnp.int32)
    own_map = lax.dynamic_slice_in_dim(sample_map, own_device * SAMP_DEV, SAMP_DEV)
    dest_dp = own_map // SAMP_DEV // expert_count
    onehot_dest = (dest_dp[:, None] == jnp.arange(dp_count, dtype=jnp.int32)[None, :]).astype(
        jnp.int32
    )
    slot_index = (jnp.cumsum(onehot_dest, axis=0) - onehot_dest)[sample_ids, dest_dp]
    empty_slots = jnp.zeros((dp_count, cap_slots, ROWS, feature_width), jnp.bfloat16)
    send_in = empty_slots.at[dest_dp, slot_index].set(
        in_cache[0].reshape(SAMP_DEV, ROWS, feature_width)
    )
    send_out = empty_slots.at[dest_dp, slot_index].set(
        out_cache[0].reshape(SAMP_DEV, ROWS, feature_width)
    )
    got_in, got_out = (
        lax.all_to_all(send_in, "dp", split_axis=0, concat_axis=0, tiled=True),
        lax.all_to_all(send_out, "dp", split_axis=0, concat_axis=0, tiled=True),
    )
    total_samples = sample_map.shape[0]
    inverse = (
        jnp.zeros((total_samples,), jnp.int32)
        .at[sample_map]
        .set(jnp.arange(total_samples, dtype=jnp.int32))
    )
    own_sources = lax.dynamic_slice_in_dim(inverse, own_device * SAMP_DEV, SAMP_DEV)
    source_device = own_sources // SAMP_DEV
    source_dp = source_device // expert_count
    source_local = own_sources % SAMP_DEV
    source_maps = sample_map.reshape(group_size, SAMP_DEV)[source_device]
    goes_here = source_maps // SAMP_DEV // expert_count == own_dp
    earlier = sample_ids[None, :] < source_local[:, None]
    arrival_slot = jnp.sum((goes_here & earlier).astype(jnp.int32), axis=1)
    in_moved = got_in[source_dp, arrival_slot].reshape(tok_rows, feature_width)
    out_moved = got_out[source_dp, arrival_slot].reshape(tok_rows, feature_width)
    tokens = inputs[0]
    flat_experts = routing[0].reshape(-1)
    sorted_order = jnp.argsort(flat_experts, stable=True)
    per_expert = tok_rows * TOPK // EXPERTS
    grouped = tokens[sorted_order // TOPK].reshape(EXPERTS, 1, per_expert, feature_width)
    outgoing = jnp.broadcast_to(grouped, (EXPERTS, slice_count, per_expert, feature_width)).reshape(
        group_size, per_expert, feature_width
    )
    up_slice = w_up[0]
    down_slice = w_down[0]
    arrived = lax.all_to_all(outgoing, ("dp", "expert"), split_axis=0, concat_axis=0, tiled=True)
    flat_rows = arrived.reshape(-1, feature_width)
    hidden = jax.nn.silu(jnp.dot(flat_rows, up_slice, preferred_element_type=jnp.float32)).astype(
        jnp.bfloat16
    )
    partial_value = jnp.dot(hidden, down_slice, preferred_element_type=jnp.float32).astype(
        jnp.bfloat16
    )
    returned = lax.all_to_all(
        partial_value.reshape(arrived.shape),
        ("dp", "expert"),
        split_axis=0,
        concat_axis=0,
        tiled=True,
    )
    summed = jnp.sum(
        returned.astype(jnp.float32).reshape(EXPERTS, slice_count, per_expert, feature_width),
        axis=1,
    )
    summed = summed.reshape(-1, feature_width)
    position = (
        jnp.zeros_like(sorted_order)
        .at[sorted_order]
        .set(jnp.arange(sorted_order.shape[0], dtype=jnp.int32))
    )
    per_assign = summed[position].reshape(tok_rows, TOPK, feature_width)
    weights = gate_table[0].astype(jnp.float32)
    weights = weights / jnp.sum(weights, axis=1, keepdims=True)
    mixed = jnp.sum(weights[:, :, None] * per_assign, axis=1)
    row_numbers = jnp.arange(tok_rows, dtype=jnp.int32) % ROWS
    valid_rows = row_numbers < jnp.repeat(lengths, ROWS)
    delta_rows = jnp.where(
        valid_rows[:, None],
        (mixed - out_moved.astype(jnp.float32)).astype(jnp.bfloat16),
        jnp.zeros((), jnp.bfloat16),
    )
    new_out = (out_moved.astype(jnp.float32) + delta_rows.astype(jnp.float32)).astype(jnp.bfloat16)
    received = from_behind(delta_rows, "section", 1)
    next_input = (in_moved.astype(jnp.float32) + received.astype(jnp.float32)).astype(jnp.bfloat16)
    return (next_input[None], new_out[None])


def solution(mesh):
    placed = (
        P("section", ("dp", "expert"), None),
        P("section", ("dp", "expert"), None),
        P("section", ("dp", "expert"), None),
        P("section", None, ("dp", "expert")),
        P("section", ("dp", "expert"), None),
        P("section", ("dp", "expert"), None),
        P("section", ("dp", "expert"), None),
        P(("dp", "expert")),
        P(),
    )
    return jax.shard_map(
        per_device,
        mesh=mesh,
        in_specs=placed,
        out_specs=(P("section", ("dp", "expert"), None), P("section", ("dp", "expert"), None)),
        check_vma=False,
    )
```

profile of v0, /device:TPU:1, one launch (start us, length us, event | category | flops | bytes accessed | tf_op | source)
XLA Modules:
  0.0 474.1 jit_solution(3733831911946649656)
XLA Ops:
  0.6 0.0 copy-start
  0.6 0.8 copy.15
  1.5 0.1 reshape_squeeze.10
  1.6 3.2 sort.17
  4.8 0.0 copy-done
  4.8 1.4 gather_fusion.3
  6.2 4.3 broadcast_in_dim.78
  10.5 0.0 copy-start.3
  10.5 0.0 copy-start.1
  10.5 13.3 %all-to-all-start.1 = ((bf16[64,32,2048]{2,1,0:T(8,128)(2,1)}), bf16[64,32,2048]{2,1,0:T(8,128)(2,1)}, u32[]{:S(2)}, u32[]{:S(2)}) async-start(bf16[64,32,2048]{2,1,0:T(8,128)(2,1)} %bitcast.85), calls=%async_computation.1 | async-start | bytes 16777216 | tf_op jit(solution)/shard_map/all_to_all | solution.py:72
  23.8 0.0 copy-done.3
  23.8 0.1 or_bitcast_fusion
  23.9 0.1 fusion.18
  24.0 0.1 fusion.22
  24.1 0.6 gather_fusion
  24.7 1.1 broadcast.218.clone
  25.8 0.0 copy-done.1
  25.8 2.5 scatter_fusion.1
  28.3 178.3 %all-to-all-done.1 = bf16[64,32,2048]{2,1,0:T(8,128)(2,1)} async-done(((bf16[64,32,2048]{2,1,0:T(8,128)(2,1)}), bf16[64,32,2048]{2,1,0:T(8,128)(2,1)}, u32[]{:S(2)}, u32[]{:S(2)}) %all-to-all-start.1) | async-done | bytes 8388640 | tf_op jit(solution)/shard_map/all_to_all | solution.py:72
  206.6 7.3 %all-to-all-start.3 = ((bf16[16,1,16,2048]{3,2,1,0:T(8,128)(2,1)}), bf16[16,1,16,2048]{3,2,1,0:T(8,128)(2,1)S(1)}, u32[]{:S(2)}, u32[]{:S(2)}) async-start(bf16[16,1,16,2048]{3,2,1,0:T(8,128)(2,1)} %bitcast.22), calls=%async_computation.3 | async-start | bytes 2097152 | tf_op jit(solution)/shard_map/all_to_all | solution.py:44
  214.0 24.3 %convolution_convert_fusion = bf16[2048,2048]{1,0:T(8,128)(2,1)} fusion(bf16[1,896,2048]{2,1,0:T(8,128)(2,1)} %param.13, bf16[2048,2048]{1,0:T(8,128)(2,1)} %bitcast.14, bf16[1,2048,896]{2,1,0:T(8,128)(2,1)} %param.12), kind=kOutput, calls=%fused_computation.11 | convolution fusion | flops 15045754880 | bytes 24117248 | tf_op jit(solution)/shard_map/dot_general | solution.py:77
  238.2 3.7 all-to-all-done.3
  241.9 0.0 copy-start.4
  241.9 0.0 copy-start.5
  242.0 0.0 copy-start.2
  242.0 7.3 %all-to-all-start.2 = ((bf16[64,32,2048]{2,1,0:T(8,128)(2,1)}), bf16[64,32,2048]{2,1,0:T(8,128)(2,1)}, u32[]{:S(2)}, u32[]{:S(2)}) async-start(bf16[64,32,2048]{2,1,0:T(8,128)(2,1)} %bitcast.86), calls=%async_computation.2 | async-start | bytes 16777216 | tf_op jit(solution)/shard_map/all_to_all | solution.py:80
  249.3 0.1 reshape.156
  249.4 0.0 copy-done.4
  249.4 0.1 copy.14
  249.5 0.0 copy-done.5
  249.5 0.1 broadcast_in_dim.74
  249.6 0.1 reshape.157
  249.7 1.6 scatter_custom_fusion.2
  251.3 2.4 scatter_custom_fusion.1
  253.8 0.1 and_select_fusion.2
  253.8 0.1 compare_select_fusion.8
  253.9 0.6 gather_fusion.1
  254.5 1.1 broadcast.218.clone.1
  255.6 0.0 copy-done.2
  255.6 2.5 scatter_fusion
  258.1 174.0 %all-to-all-done.2 = bf16[64,32,2048]{2,1,0:T(8,128)(2,1)} async-done(((bf16[64,32,2048]{2,1,0:T(8,128)(2,1)}), bf16[64,32,2048]{2,1,0:T(8,128)(2,1)}, u32[]{:S(2)}, u32[]{:S(2)}) %all-to-all-start.2) | async-done | bytes 8388640 | tf_op jit(solution)/shard_map/all_to_all | solution.py:80
  432.1 7.3 %all-to-all-start = ((bf16[16,1,16,2048]{3,2,1,0:T(8,128)(2,1)}), bf16[16,1,16,2048]{3,2,1,0:T(8,128)(2,1)}, u32[]{:S(2)}, u32[]{:S(2)}) async-start(bf16[16,1,16,2048]{3,2,1,0:T(8,128)(2,1)} %bitcast.5), calls=%async_computation | async-start | bytes 2097152 | tf_op jit(solution)/shard_map/all_to_all | solution.py:43
  439.5 0.2 convert_reduce_fusion.1
  439.7 0.6 gather_fusion.5
  440.3 5.4 %convert_reduce_fusion = f32[8,32,2048]{2,1,0:T(8,128)S(1)} fusion(bf16[64,32,2048]{2,1,0:T(8,128)(2,1)} %all-to-all-done.2), kind=kLoop, calls=%fused_computation.10 | loop fusion | flops 7864320 | bytes 10485760 | tf_op jit(solution)/shard_map/reduce_sum | solution.py:87
  445.7 2.7 gather_fusion.4
  448.4 3.5 reshape.164
  451.8 4.7 multiply_reduce_fusion
  456.6 0.9 fusion.12
  457.5 4.0 collective-permute-start
  461.5 0.1 convert_element_type.105
  461.6 5.9 %all-to-all-done = bf16[16,1,16,2048]{3,2,1,0:T(8,128)(2,1)} async-done(((bf16[16,1,16,2048]{3,2,1,0:T(8,128)(2,1)}), bf16[16,1,16,2048]{3,2,1,0:T(8,128)(2,1)}, u32[]{:S(2)}, u32[]{:S(2)}) %all-to-all-start) | async-done | bytes 1048608 | tf_op jit(solution)/shard_map/all_to_all | solution.py:43
  467.5 1.8 gather_fusion.2
  469.4 1.1 fusion.10
  470.5 1.7 collective-permute-done
  472.1 2.0 fusion.14
  (15 shorter events, 0.1 us)
Async XLA Ops:
  0.6 4.2 copy-start
  10.5 13.3 %copy-start.3 = (s32[512]{0:T(512)S(1)}, s32[512]{0:T(512)}, u32[]{:S(2)}) copy-start(s32[512]{0:T(512)} %param.17) | copy-start | bytes 6148
  10.5 15.4 %copy-start.1 = (bf16[1,128,2048]{2,1,0:T(8,128)(2,1)S(1)}, bf16[1,128,2048]{2,1,0:T(8,128)(2,1)}, u32[]{:S(2)}) copy-start(bf16[1,128,2048]{2,1,0:T(8,128)(2,1)} %param.11) | copy-start | bytes 1572868
  10.5 196.1 %all-to-all-start.1 = ((bf16[64,32,2048]{2,1,0:T(8,128)(2,1)}), bf16[64,32,2048]{2,1,0:T(8,128)(2,1)}, u32[]{:S(2)}, u32[]{:S(2)}) async-start(bf16[64,32,2048]{2,1,0:T(8,128)(2,1)} %bitcast.85), calls=%async_computation.1 | async-start | bytes 16777216 | tf_op jit(solution)/shard_map/all_to_all | solution.py:72
  206.6 35.3 %all-to-all-start.3 = ((bf16[16,1,16,2048]{3,2,1,0:T(8,128)(2,1)}), bf16[16,1,16,2048]{3,2,1,0:T(8,128)(2,1)S(1)}, u32[]{:S(2)}, u32[]{:S(2)}) async-start(bf16[16,1,16,2048]{3,2,1,0:T(8,128)(2,1)} %bitcast.22), calls=%async_computation.3 | async-start | bytes 2097152 | tf_op jit(solution)/shard_map/all_to_all | solution.py:44
  241.9 7.4 %copy-start.4 = (s32[1,128,2]{1,2,0:T(2,128)S(1)}, s32[1,128,2]{1,2,0:T(2,128)}, u32[]{:S(2)}) copy-start(s32[1,128,2]{1,2,0:T(2,128)} %param.15) | copy-start | bytes 3076
  241.9 7.6 %copy-start.5 = (s32[8]{0:T(128)S(1)}, s32[8]{0:T(128)}, u32[]{:S(2)}) copy-start(s32[8]{0:T(128)} %param.16) | copy-start | bytes 100
  242.0 13.7 %copy-start.2 = (bf16[1,128,2048]{2,1,0:T(8,128)(2,1)S(1)}, bf16[1,128,2048]{2,1,0:T(8,128)(2,1)}, u32[]{:S(2)}) copy-start(bf16[1,128,2048]{2,1,0:T(8,128)(2,1)} %param.10) | copy-start | bytes 1572868
  242.0 190.2 %all-to-all-start.2 = ((bf16[64,32,2048]{2,1,0:T(8,128)(2,1)}), bf16[64,32,2048]{2,1,0:T(8,128)(2,1)}, u32[]{:S(2)}, u32[]{:S(2)}) async-start(bf16[64,32,2048]{2,1,0:T(8,128)(2,1)} %bitcast.86), calls=%async_computation.2 | async-start | bytes 16777216 | tf_op jit(solution)/shard_map/all_to_all | solution.py:80
  432.1 35.4 %all-to-all-start = ((bf16[16,1,16,2048]{3,2,1,0:T(8,128)(2,1)}), bf16[16,1,16,2048]{3,2,1,0:T(8,128)(2,1)}, u32[]{:S(2)}, u32[]{:S(2)}) async-start(bf16[16,1,16,2048]{3,2,1,0:T(8,128)(2,1)} %bitcast.5), calls=%async_computation | async-start | bytes 2097152 | tf_op jit(solution)/shard_map/all_to_all | solution.py:43
  457.5 14.6 %collective-permute-start = (bf16[128,2048]{1,0:T(8,128)(2,1)}, bf16[128,2048]{1,0:T(8,128)(2,1)}, u32[]{:S(2)}, u32[]{:S(2)}) collective-permute-start(bf16[128,2048]{1,0:T(8,128)(2,1)} %fusion.12), channel_id=1, source_target_pairs={{0,64},{64,128},{128,192},{1,65},{65,129},{129,193},{2,66},{66,130... | collective-permute-start | bytes 1572872 | tf_op jit(solution)/shard_map/ppermute | solution.py:15
where the time goes:
time: 476 us; the launch traced here: 474 us
  waiting for transfers between devices  364 us (76%)
  starting transfers between devices  39.3 us (8%)
  local copies, waits for them, and re-layouts  27.9 us (6%)
  matrix products  24.3 us (5%)
  other arithmetic  18.1 us (4%)
    all_to_all x1, waiting for transfers between devices, per_device(): lax.all_to_all(outgoing, ('dp', 'expert'), split_axis=0, concat_axis=0, t...  178 us
    all_to_all x1, waiting for transfers between devices, per_device(): lax.all_to_all(partial_value.reshape(arrived.shape), ('dp', 'expert'), sp...  174 us
    dot_general x1, matrix products, per_device(): jnp.dot(hidden, down_slice, preferred_element_type=jnp.float32)  24.3 us
    all_to_all x1, starting transfers between devices, per_device(): lax.all_to_all(outgoing, ('dp', 'expert'), split_axis=0, concat_axis=0, t...  13.3 us
  transfers between devices with their start and end apart: 5, of which 5 were waited for; matrix products, arithmetic and copies ran while one was open for 12% of the time, Pallas kernels for 0%

commit v1 on v0

v1 whole, which is shorter than its diff:
```python
import functools

import jax
import jax.numpy as jnp
from jax import lax
from jax.experimental import pallas as pl
from jax.experimental.pallas import tpu as pltpu
from jax.sharding import Mesh, PartitionSpec as P

EXPERTS = 8
TOPK = 2
ROWS = 16
SAMP_DEV = 8
BF16 = jnp.bfloat16
F32 = jnp.float32


def shifted(value, axis, by):
    peers = lax.axis_size(axis)
    return lax.ppermute(value, axis, [(i, (i + by) % peers) for i in range(peers)])


def group_kernel(routing_ref, tokens_ref, grouped_ref, slot_ref):
    rows = routing_ref.shape[0]
    slots = grouped_ref.shape[0]
    per_expert = slots // EXPERTS
    routing = routing_ref[...]
    lanes = lax.broadcasted_iota(jnp.int32, (rows, rows), 1)
    earlier = (lax.broadcasted_iota(jnp.int32, (rows, rows), 0) > lanes).astype(BF16)
    first = (routing[:, 0:1] == lanes).astype(F32)
    second = (routing[:, 1:2] == lanes).astype(F32)
    before_first = jnp.dot(earlier, first.astype(BF16), preferred_element_type=F32)
    before_second = jnp.dot(earlier, second.astype(BF16), preferred_element_type=F32) + jnp.sum(
        first, axis=0, keepdims=True
    )
    base = (lanes * per_expert).astype(F32)
    slot_first = jnp.sum(first * (before_first + base), axis=1, keepdims=True).astype(jnp.int32)
    slot_second = jnp.sum(second * (before_second + base), axis=1, keepdims=True).astype(jnp.int32)
    slot_lanes = lax.broadcasted_iota(jnp.int32, (rows, slots), 1)
    chosen = ((slot_first == slot_lanes) | (slot_second == slot_lanes)).astype(F32).astype(BF16)
    grouped_ref[...] = lax.dot_general(
        chosen, tokens_ref[...], (((0,), (0,)), ((), ())), preferred_element_type=F32
    ).astype(BF16)
    slot_ref[:, 0:1] = slot_first
    slot_ref[:, 1:2] = slot_second


def group_rows(routing, tokens):
    rows, width = tokens.shape
    slots = rows * TOPK
    return pl.pallas_call(
        group_kernel,
        out_shape=(
            jax.ShapeDtypeStruct((slots, width), BF16),
            jax.ShapeDtypeStruct((rows, TOPK), jnp.int32),
        ),
        cost_estimate=pl.CostEstimate(
            flops=2 * slots * rows * width, bytes_accessed=3 * slots * width, transcendentals=0
        ),
        name="group_rows",
    )(routing, tokens)


def combine_kernel(back_ref, slot_ref, gate_ref, live_ref, moved_ref, delta_ref, cache_ref):
    rows = slot_ref.shape[0]
    slots = back_ref.shape[0]
    slot_lanes = lax.broadcasted_iota(jnp.int32, (rows, slots), 1)
    slot = slot_ref[...]
    back = back_ref[...]
    pick_first = (slot[:, 0:1] == slot_lanes).astype(F32).astype(BF16)
    pick_second = (slot[:, 1:2] == slot_lanes).astype(F32).astype(BF16)
    first = jnp.dot(pick_first, back, preferred_element_type=F32)
    second = jnp.dot(pick_second, back, preferred_element_type=F32)
    gates = gate_ref[...].astype(F32)
    total = gates[:, 0:1] + gates[:, 1:2]
    mixed = gates[:, 0:1] / total * first + gates[:, 1:2] / total * second
    moved = moved_ref[...].astype(F32)
    delta = jnp.where(live_ref[...] > 0, mixed - moved, 0.0).astype(BF16)
    delta_ref[...] = delta
    cache_ref[...] = (moved + delta.astype(F32)).astype(BF16)


def combine(back, slot, gates, live, moved):
    rows, width = moved.shape
    out = jax.ShapeDtypeStruct((rows, width), BF16)
    return pl.pallas_call(
        combine_kernel,
        out_shape=(out, out),
        cost_estimate=pl.CostEstimate(
            flops=4 * back.shape[0] * rows * width,
            bytes_accessed=2 * back.size + 6 * moved.size,
            transcendentals=0,
        ),
        name="combine",
    )(back, slot, gates, live, moved)


def per_device(
    inputs, in_cache, out_cache, w_up, w_down, routing, gate_table, lengths, sample_map
):
    width = inputs.shape[2]
    tok_rows = inputs.shape[1]
    z_count = lax.axis_size("z")
    x_count = lax.axis_size("x")
    dp_count = z_count * lax.axis_size("core")
    own_dp = lax.axis_index(("z", "core"))
    own_device = own_dp * x_count + lax.axis_index("x")

    grouped, slot = group_rows(routing[0], inputs[0])
    up_own, down_own = w_up[0], w_down[0]
    up_other = shifted(up_own, "core", 1)
    down_other = shifted(down_own, "core", 1)
    block = lax.all_to_all(
        grouped.reshape(z_count, -1, width), "z", split_axis=0, concat_axis=0, tiled=True
    ).reshape(-1, width)
    half = block.shape[0] // 2
    from_left = shifted(block, "x", 1)
    from_right = shifted(block, "x", -1)
    far_top = shifted(from_left[:half], "x", 1)
    far_bottom = shifted(from_right[half:], "x", -1)

    def expert(rows):
        hidden_own = jax.nn.silu(jnp.dot(rows, up_own, preferred_element_type=F32)).astype(BF16)
        hidden_other = jax.nn.silu(jnp.dot(rows, up_other, preferred_element_type=F32)).astype(BF16)
        return (
            jnp.dot(hidden_own, down_own, preferred_element_type=F32)
            + jnp.dot(hidden_other, down_other, preferred_element_type=F32)
        ).astype(BF16)

    out_own = expert(block)
    out_left = expert(from_left)
    out_right = expert(from_right)
    out_far_top = expert(far_top)
    out_far_bottom = expert(far_bottom)

    top = shifted(out_far_top, "x", -1)
    bottom = shifted(out_far_bottom, "x", 1)
    to_left = jnp.concatenate(
        [(out_left[:half].astype(F32) + top.astype(F32)).astype(BF16), out_left[half:]]
    )
    to_right = jnp.concatenate(
        [out_right[:half], (out_right[half:].astype(F32) + bottom.astype(F32)).astype(BF16)]
    )
    got_right = shifted(to_left, "x", -1)
    got_left = shifted(to_right, "x", 1)
    summed = (
        out_own.astype(F32) + got_right.astype(F32) + got_left.astype(F32)
    ).astype(BF16)
    back = lax.all_to_all(
        summed.reshape(z_count, -1, width), "z", split_axis=0, concat_axis=0, tiled=True
    ).reshape(-1, width)

    own_map = lax.dynamic_slice_in_dim(sample_map, own_device * SAMP_DEV, SAMP_DEV)
    dest_dp = own_map // SAMP_DEV // x_count
    sample_ids = jnp.arange(SAMP_DEV, dtype=jnp.int32)
    goes = dest_dp[None, :] == jnp.arange(dp_count, dtype=jnp.int32)[:, None]
    slot_sample = jnp.sum(jnp.where(goes, sample_ids[None, :], 0), axis=1)
    own_places = own_device * SAMP_DEV + sample_ids
    sources = jnp.sum(
        jnp.where(
            sample_map[None, :] == own_places[:, None],
            jnp.arange(sample_map.shape[0], dtype=jnp.int32)[None, :],
            0,
        ),
        axis=1,
    )
    source_dp = sources // SAMP_DEV // x_count

    def migrate(cache):
        sent = cache.reshape(SAMP_DEV, ROWS, width)[slot_sample]
        got = lax.all_to_all(sent, ("z", "core"), split_axis=0, concat_axis=0, tiled=True)
        return got[source_dp].reshape(tok_rows, width)

    out_moved = migrate(out_cache[0])
    in_moved = migrate(in_cache[0])

    live = (
        jnp.arange(tok_rows, dtype=jnp.int32) % ROWS < jnp.repeat(lengths, ROWS)
    ).astype(jnp.int32)[:, None]
    delta, new_out = combine(back, slot, gate_table[0], live, out_moved)
    sections = lax.axis_size("section")
    received = lax.ppermute(delta, "section", [(i, i + 1) for i in range(sections - 1)])
    next_input = (in_moved.astype(F32) + received.astype(F32)).astype(BF16)
    return next_input[None], new_out[None]


def solution(mesh):
    sections, dp, expert = mesh.devices.shape
    split = Mesh(
        mesh.devices.reshape(sections, dp // 2, 2, expert), ("section", "z", "core", "x")
    )
    group = ("z", "core", "x")
    rows = P("section", group, None)
    placed = (rows, rows, rows, P("section", None, group), rows, rows, rows, P(group), P())
    return jax.shard_map(
        per_device, mesh=split, in_specs=placed, out_specs=(rows, rows), check_vma=False
    )
```

time: 476 us -> 233 us (0.49)
  waiting for transfers between devices: 364 us -> 103 us
  matrix products: 24.3 us -> 63.9 us
  local copies, waits for them, and re-layouts: 27.9 us -> 13.7 us
  other arithmetic: 18.1 us -> 7.43 us
  Pallas kernels: 0 us -> 6.09 us
    all_to_all x4, waiting for transfers between devices: 362 us -> 70.8 us  [the longest x1 28.1 us: per_device(): lax.all_to_all(grouped.reshape(z_count, -1, width), 'z', split_axis=0, co...]
    dot_general x1 -> x10, matrix products: 24.3 us -> 63.9 us  [the longest x5 32.1 us: expert(): jnp.dot(hidden_other, down_other, preferred_element_type=F32)]
    ppermute x1 -> x11, waiting for transfers between devices: 1.66 us -> 31.7 us  [the longest x10 31.7 us: shifted(): lax.ppermute(value, axis, [(i, (i + by) % peers) for i in range(peers)])]
    all_to_all x4, starting transfers between devices: 35.3 us -> 25.1 us  [the longest x2 12.4 us: migrate(): lax.all_to_all(sent, ('z', 'core'), split_axis=0, concat_axis=0, tiled=True)]
    reduce_sum x4 -> x2, other arithmetic: 10.3 us -> 0.27 us  [the longest x1 0.18 us: per_device(): jnp.sum(jnp.where(sample_map[None, :] == own_places[:, None], jnp.arange(...]
    scatter x4 -> x0, local copies, waits for them, and re-layouts: 8.95 us -> none  [the longest x2 4.93 us: per_device(): empty_slots.at[dest_dp, slot_index]]
    ppermute x1 -> x11, starting transfers between devices: 3.99 us -> 12.6 us  [the longest x10 9.34 us: shifted(): lax.ppermute(value, axis, [(i, (i + by) % peers) for i in range(peers)])]
    broadcast_in_dim x4 -> x1, local copies, waits for them, and re-layouts: 6.59 us -> 0.07 us  [per_device(): jnp.repeat(lengths, ROWS)]
  transfers between devices with their start and end apart: 5 -> 15, of which waited for: 5 -> 7; matrix products, arithmetic and copies ran while one was open for 12% -> 35% of each run, Pallas kernels for 0% -> 1%
where the time goes in v1:
time: 233 us; the launch traced here: 232 us
  waiting for transfers between devices  103 us (44%)
  matrix products  63.9 us (27%)
  starting transfers between devices  37.7 us (16%)
  local copies, waits for them, and re-layouts  13.7 us (6%)
  other arithmetic  7.43 us (3%)
  Pallas kernels  6.09 us (3%)
    dot_general x5, matrix products, expert(): jnp.dot(hidden_other, down_other, preferred_element_type=F32)  32.1 us
    dot_general x5, matrix products, expert(): jnp.dot(hidden_own, down_own, preferred_element_type=F32)  31.8 us
    ppermute x10, waiting for transfers between devices, shifted(): lax.ppermute(value, axis, [(i, (i + by) % peers) for i in range(peers)])  31.7 us
    all_to_all x1, waiting for transfers between devices, per_device(): lax.all_to_all(grouped.reshape(z_count, -1, width), 'z', split_axis=0, co...  28.1 us
    all_to_all x1, waiting for transfers between devices, per_device(): lax.all_to_all(summed.reshape(z_count, -1, width), 'z', split_axis=0, con...  24.2 us
    all_to_all x2, waiting for transfers between devices, migrate(): lax.all_to_all(sent, ('z', 'core'), split_axis=0, concat_axis=0, tiled=True)  18.5 us
    all_to_all x2, starting transfers between devices, migrate(): lax.all_to_all(sent, ('z', 'core'), split_axis=0, concat_axis=0, tiled=True)  12.4 us
    ppermute x10, starting transfers between devices, shifted(): lax.ppermute(value, axis, [(i, (i + by) % peers) for i in range(peers)])  9.34 us
  transfers between devices with their start and end apart: 15, of which 7 were waited for; matrix products, arithmetic and copies ran while one was open for 35% of the time, Pallas kernels for 1%

profile of v1, /device:TPU:1, one launch (start us, length us, event | category | flops | bytes accessed | tf_op | source)
XLA Modules:
  0.0 232.1 jit_solution(17111178003806759728)
XLA Ops:
  0.6 0.0 copy-start
  0.6 1.5 copy.17
  2.1 2.9 %group_rows.1 = (bf16[256,2048]{1,0:T(8,128)(2,1)}, s32[128,2]{1,0:T(8,128)}) custom-call(s32[128,2]{1,0:T(8,128)} %bitcast.106, bf16[128,2048]{1,0:T(8,128)(2,1)} %bitcast.104), custom_call_target="tpu_custom_call" | custom-call | flops 134217728 | bytes 1572864 | tf_op jit(solution)/shard_map/group_rows/pallas_call | solution.py:51
  5.1 9.0 %all-to-all-start.1 = ((bf16[8,32,2048]{2,1,0:T(8,128)(2,1)}), bf16[8,32,2048]{2,1,0:T(8,128)(2,1)S(1)}, u32[]{:S(2)}, u32[]{:S(2)}) async-start(bf16[8,32,2048]{2,1,0:T(8,128)(2,1)} %bitcast.103), calls=%async_computation.1 | async-start | bytes 2097152 | tf_op jit(solution)/shard_map/all_to_all | solution.py:113
  14.1 1.0 collective-permute-start
  15.0 0.1 collective-permute-start.1
  15.1 28.1 %all-to-all-done.1 = bf16[8,32,2048]{2,1,0:T(8,128)(2,1)S(1)} async-done(((bf16[8,32,2048]{2,1,0:T(8,128)(2,1)}), bf16[8,32,2048]{2,1,0:T(8,128)(2,1)S(1)}, u32[]{:S(2)}, u32[]{:S(2)}) %all-to-all-start.1) | async-done | bytes 1048608 | tf_op jit(solution)/shard_map/all_to_all | solution.py:113
  43.3 1.2 collective-permute-start.2
  44.5 1.5 collective-permute-start.6
  45.9 0.8 and_select_fusion.3
  46.7 0.1 select_reduce_fusion.1
  46.8 1.6 gather_fusion.2
  48.4 4.5 %all-to-all-start.3 = ((bf16[16,16,2048]{2,1,0:T(8,128)(2,1)}), bf16[16,16,2048]{2,1,0:T(8,128)(2,1)S(1)}, u32[]{:S(2)}, u32[]{:S(2)}) async-start(bf16[16,16,2048]{2,1,0:T(8,128)(2,1)} %gather_fusion.2), calls=%async_computation.3 | async-start | bytes 2097152 | tf_op jit(solution)/shard_map/all_to_all | solution.py:171
  52.9 15.9 %collective-permute-done.2 = bf16[256,2048]{1,0:T(8,128)(2,1)} collective-permute-done((bf16[256,2048]{1,0:T(8,128)(2,1)S(1)}, bf16[256,2048]{1,0:T(8,128)(2,1)}, u32[]{:S(2)}, u32[]{:S(2)}) %collective-permute-start.2) | collective-permute-done | bytes 1048608 | tf_op jit(solution)/shard_map/ppermute | solution.py:20
  68.8 1.9 slice.33
  70.7 0.0 collective-permute-start.3
  70.7 0.0 collective-permute-done.6
  70.7 1.9 slice.37
  72.6 2.7 %collective-permute-start.7 = (bf16[128,2048]{1,0:T(8,128)(2,1)}, bf16[128,2048]{1,0:T(8,128)(2,1)S(1)}, u32[]{:S(2)}, u32[]{:S(2)}) collective-permute-start(bf16[128,2048]{1,0:T(8,128)(2,1)} %slice.37), channel_id=1, source_target_pairs={{0,3},{1,0},{2,1},{3,2},{4,7},{5,4},{6,5},{7,6},{8,11},{9,8},{10,9... | collective-permute-start | bytes 1572872 | tf_op jit(solution)/shard_map/ppermute | solution.py:20
  75.2 7.1 %fusion.12 = f32[256,2048]{1,0:T(8,128)} fusion(bf16[1,896,2048]{2,1,0:T(8,128)(2,1)} %param.13, bf16[256,2048]{1,0:T(8,128)(2,1)} %collective-permute-done.2, bf16[1,2048,896]{2,1,0:T(8,128)(2,1)} %param.12), kind=kOutput, calls=%fused_computation.32 | convolution fusion | flops 1880195072 | bytes 10485760 | tf_op jit(solution)/shard_map/dot_general | solution.py:126
  82.4 7.2 %fusion.13 = f32[256,2048]{1,0:T(8,128)} fusion(bf16[1,896,2048]{2,1,0:T(8,128)(2,1)} %param.13, bf16[256,2048]{1,0:T(8,128)(2,1)} %collective-permute-done.6, bf16[1,2048,896]{2,1,0:T(8,128)(2,1)} %param.12), kind=kOutput, calls=%fused_computation.33 | convolution fusion | flops 1880195072 | bytes 10485760 | tf_op jit(solution)/shard_map/dot_general | solution.py:126
  89.6 0.0 collective-permute-done.3
  89.6 4.7 %fusion.20 = f32[128,2048]{1,0:T(8,128)S(1)} fusion(bf16[1,896,2048]{2,1,0:T(8,128)(2,1)} %param.13, bf16[128,2048]{1,0:T(8,128)(2,1)} %collective-permute-done.3, bf16[1,2048,896]{2,1,0:T(8,128)(2,1)} %param.12), kind=kOutput, calls=%fused_computation.44 | convolution fusion | flops 940097536 | bytes 8912896 | tf_op jit(solution)/shard_map/dot_general | solution.py:126
  94.3 0.0 collective-permute-done.7
  94.3 5.5 %fusion.21 = f32[128,2048]{1,0:T(8,128)} fusion(bf16[1,896,2048]{2,1,0:T(8,128)(2,1)} %param.13, bf16[128,2048]{1,0:T(8,128)(2,1)S(1)} %collective-permute-done.7, bf16[1,2048,896]{2,1,0:T(8,128)(2,1)} %param.12), kind=kOutput, calls=%fused_computation.45 | convolution fusion | flops 940097536 | bytes 8912896 | tf_op jit(solution)/shard_map/dot_general | solution.py:126
  99.8 0.0 collective-permute-done
  99.8 0.0 collective-permute-done.1
  99.8 5.5 %fusion.7 = bf16[128,2048]{1,0:T(8,128)(2,1)} fusion(f32[128,2048]{1,0:T(8,128)S(1)} %fusion.20, bf16[896,2048]{1,0:T(8,128)(2,1)} %collective-permute-done.1, bf16[128,2048]{1,0:T(8,128)(2,1)} %collective-permute-done.3, bf16[2048,896]{1,0:T(8,128)(2,1)} %collective-permute-done), kind=kOutput, calls=%fused_computation.16 | convolution fusion | flops 940621824 | bytes 9437184 | tf_op jit(solution)/shard_map/dot_general | solution.py:127
  105.3 0.1 collective-permute-start.4
  105.3 6.4 %fusion.5 = bf16[256,2048]{1,0:T(8,128)(2,1)S(1)} fusion(f32[256,2048]{1,0:T(8,128)} %fusion.12, bf16[896,2048]{1,0:T(8,128)(2,1)} %collective-permute-done.1, bf16[256,2048]{1,0:T(8,128)(2,1)} %collective-permute-done.2, bf16[2048,896]{1,0:T(8,128)(2,1)} %collective-permute-done), kind=kOutput, calls=%fused_computation.12 | convolution fusion | flops 1881243648 | bytes 11534336 | tf_op jit(solution)/shard_map/dot_general | solution.py:127
  111.8 5.9 %fusion.8 = bf16[128,2048]{1,0:T(8,128)(2,1)} fusion(f32[128,2048]{1,0:T(8,128)} %fusion.21, bf16[896,2048]{1,0:T(8,128)(2,1)} %collective-permute-done.1, bf16[128,2048]{1,0:T(8,128)(2,1)S(1)} %collective-permute-done.7, bf16[2048,896]{1,0:T(8,128)(2,1)} %collective-permute-done), kind=kOutput, calls=%fused_computation.17 | convolution fusion | flops 940621824 | bytes 9437184 | tf_op jit(solution)/shard_map/dot_general | solution.py:127
  117.7 1.4 collective-permute-start.8
  119.1 6.5 %fusion.6 = bf16[256,2048]{1,0:T(8,128)(2,1)S(1)} fusion(f32[256,2048]{1,0:T(8,128)} %fusion.13, bf16[896,2048]{1,0:T(8,128)(2,1)} %collective-permute-done.1, bf16[256,2048]{1,0:T(8,128)(2,1)} %collective-permute-done.6, bf16[2048,896]{1,0:T(8,128)(2,1)} %collective-permute-done), kind=kOutput, calls=%fused_computation.13 | convolution fusion | flops 1881243648 | bytes 11534336 | tf_op jit(solution)/shard_map/dot_general | solution.py:127
  125.6 1.0 copy-done.3
  126.5 0.0 collective-permute-done.4
  126.5 1.4 add_convert_fusion.1
  128.0 1.1 pad_maximum_fusion
  129.1 1.3 collective-permute-start.5
  130.3 0.2 collective-permute-done.8
  130.5 1.2 add_convert_fusion
  131.7 1.1 pad_maximum_fusion.1
  132.8 0.2 collective-permute-start.9
  133.0 7.3 %fusion.11 = f32[256,2048]{1,0:T(8,128)} fusion(bf16[1,896,2048]{2,1,0:T(8,128)(2,1)} %param.13, bf16[256,2048]{1,0:T(8,128)(2,1)} %bitcast.100, bf16[1,2048,896]{2,1,0:T(8,128)(2,1)} %param.12), kind=kOutput, calls=%fused_computation.31 | convolution fusion | flops 1880195072 | bytes 10485760 | tf_op jit(solution)/shard_map/dot_general | solution.py:126
  140.3 11.4 %collective-permute-done.5 = bf16[256,2048]{1,0:T(8,128)(2,1)} collective-permute-done((bf16[256,2048]{1,0:T(8,128)(2,1)}, bf16[256,2048]{1,0:T(8,128)(2,1)}, u32[]{:S(2)}, u32[]{:S(2)}) %collective-permute-start.5) | collective-permute-done | bytes 1048608 | tf_op jit(solution)/shard_map/ppermute | solution.py:20
  151.6 4.3 %collective-permute-done.9 = bf16[256,2048]{1,0:T(8,128)(2,1)} collective-permute-done((bf16[256,2048]{1,0:T(8,128)(2,1)}, bf16[256,2048]{1,0:T(8,128)(2,1)}, u32[]{:S(2)}, u32[]{:S(2)}) %collective-permute-start.9) | collective-permute-done | bytes 1048608 | tf_op jit(solution)/shard_map/ppermute | solution.py:20
  156.0 7.8 %fusion.4 = bf16[256,2048]{1,0:T(8,128)(2,1)} fusion(f32[256,2048]{1,0:T(8,128)} %fusion.11, bf16[896,2048]{1,0:T(8,128)(2,1)} %collective-permute-done.1, bf16[256,2048]{1,0:T(8,128)(2,1)} %collective-permute-done.9, bf16[256,2048]{1,0:T(8,128)(2,1)} %collective-permute-done.5, bf16[256,2048]{1,0:T(8,128)(2,1)S(1)} %bitcast.101, ...), kind=kOutput, calls=%fused_computation.11 | convolution fusion | flops 1884389376 | bytes 13631488 | tf_op jit(solution)/shard_map/dot_general | solution.py:127
  163.8 0.0 all-to-all-done.3
  163.8 3.7 %all-to-all-start.2 = ((bf16[8,32,2048]{2,1,0:T(8,128)(2,1)}), bf16[8,32,2048]{2,1,0:T(8,128)(2,1)S(1)}, u32[]{:S(2)}, u32[]{:S(2)}) async-start(bf16[8,32,2048]{2,1,0:T(8,128)(2,1)} %bitcast.102), calls=%async_computation.2 | async-start | bytes 2097152 | tf_op jit(solution)/shard_map/all_to_all | solution.py:149
  167.5 1.6 gather_fusion
  169.1 24.2 %all-to-all-done.2 = bf16[8,32,2048]{2,1,0:T(8,128)(2,1)S(1)} async-done(((bf16[8,32,2048]{2,1,0:T(8,128)(2,1)}), bf16[8,32,2048]{2,1,0:T(8,128)(2,1)S(1)}, u32[]{:S(2)}, u32[]{:S(2)}) %all-to-all-start.2) | async-done | bytes 1048608 | tf_op jit(solution)/shard_map/all_to_all | solution.py:149
  193.3 7.9 %all-to-all-start = ((bf16[16,16,2048]{2,1,0:T(8,128)(2,1)}), bf16[16,16,2048]{2,1,0:T(8,128)(2,1)}, u32[]{:S(2)}, u32[]{:S(2)}) async-start(bf16[16,16,2048]{2,1,0:T(8,128)(2,1)} %gather_fusion), calls=%async_computation | async-start | bytes 2097152 | tf_op jit(solution)/shard_map/all_to_all | solution.py:171
  201.2 0.1 broadcast_in_dim.48
  201.3 0.1 reshape.186
  201.4 0.1 copy.19
  201.5 0.6 convert_element_type.124.live_ref
  202.1 0.8 copy.18
  202.9 0.2 select_reduce_fusion
  203.1 1.4 gather_fusion.3
  204.5 3.1 %combine.1 = (bf16[128,2048]{1,0:T(8,128)(2,1)}, bf16[128,2048]{1,0:T(8,128)(2,1)}) custom-call(bf16[256,2048]{1,0:T(8,128)(2,1)} %bitcast.95, s32[128,2]{1,0:T(8,128)} %get-tuple-element.7.slot_ref, s32[128,2]{1,0:T(8,128)} %bitcast.105, s32[128,1]{1,0:T(8,128)} %convert_element_type.124.live_ref, bf16[128,2048]{1,0:T(8,128)(2,1)} %bitcast.97), custom_call_target="tpu_custom_call" | custom-call | flops 268435456 | bytes 2621440 | tf_op jit(solution)/shard_map/combine/pallas_call | solution.py:86
  207.6 3.2 %collective-permute-start.10 = (bf16[128,2048]{1,0:T(8,128)(2,1)}, bf16[128,2048]{1,0:T(8,128)(2,1)S(1)}, u32[]{:S(2)}, u32[]{:S(2)}) collective-permute-start(bf16[128,2048]{1,0:T(8,128)(2,1)} %get-tuple-element.8), channel_id=1, source_target_pairs={{0,64},{64,128},{128,192},{1,65},{65,129},{129,193},{2,66},{66,130... | collective-permute-start | bytes 1572872 | tf_op jit(solution)/shard_map/ppermute | solution.py:182
  210.9 18.5 %all-to-all-done = bf16[16,16,2048]{2,1,0:T(8,128)(2,1)} async-done(((bf16[16,16,2048]{2,1,0:T(8,128)(2,1)}), bf16[16,16,2048]{2,1,0:T(8,128)(2,1)}, u32[]{:S(2)}, u32[]{:S(2)}) %all-to-all-start) | async-done | bytes 1048608 | tf_op jit(solution)/shard_map/all_to_all | solution.py:171
  229.3 1.8 gather_fusion.1
  231.2 0.0 collective-permute-done.10
  231.2 1.0 fusion.10
  (30 shorter events, 0.1 us)
Async XLA Ops:
  0.6 46.2 %copy-start = (bf16[1,128,2048]{2,1,0:T(8,128)(2,1)S(1)}, bf16[1,128,2048]{2,1,0:T(8,128)(2,1)}, u32[]{:S(2)}) copy-start(bf16[1,128,2048]{2,1,0:T(8,128)(2,1)} %param.11) | copy-start | bytes 1572868
  5.1 38.2 %all-to-all-start.1 = ((bf16[8,32,2048]{2,1,0:T(8,128)(2,1)}), bf16[8,32,2048]{2,1,0:T(8,128)(2,1)S(1)}, u32[]{:S(2)}, u32[]{:S(2)}) async-start(bf16[8,32,2048]{2,1,0:T(8,128)(2,1)} %bitcast.103), calls=%async_computation.1 | async-start | bytes 2097152 | tf_op jit(solution)/shard_map/all_to_all | solution.py:113
  14.1 85.7 %collective-permute-start = (bf16[2048,896]{1,0:T(8,128)(2,1)}, bf16[2048,896]{1,0:T(8,128)(2,1)}, u32[]{:S(2)}, u32[]{:S(2)}) collective-permute-start(bf16[2048,896]{1,0:T(8,128)(2,1)} %bitcast.108), channel_id=1, source_target_pairs={{0,4},{4,0},{1,5},{5,1},{2,6},{6,2},{3,7},{7,3},{8,12},{12,8},{9,1... | collective-permute-start | bytes 11010056 | tf_op jit(solution)/shard_map/ppermute | solution.py:20
  15.0 84.8 %collective-permute-start.1 = (bf16[896,2048]{1,0:T(8,128)(2,1)}, bf16[896,2048]{1,0:T(8,128)(2,1)}, u32[]{:S(2)}, u32[]{:S(2)}) collective-permute-start(bf16[896,2048]{1,0:T(8,128)(2,1)} %bitcast.107), channel_id=1, source_target_pairs={{0,4},{4,0},{1,5},{5,1},{2,6},{6,2},{3,7},{7,3},{8,12},{12,8},{9,1... | collective-permute-start | bytes 11010056 | tf_op jit(solution)/shard_map/ppermute | solution.py:20
  43.3 39.1 %copy-start.6 = (bf16[8,32,2048]{2,1,0:T(8,128)(2,1)}, bf16[8,32,2048]{2,1,0:T(8,128)(2,1)S(1)}, u32[]{:S(2)}) copy-start(bf16[8,32,2048]{2,1,0:T(8,128)(2,1)S(1)} %all-to-all-done.1) | copy-start | bytes 3145732
  43.3 25.5 %collective-permute-start.2 = (bf16[256,2048]{1,0:T(8,128)(2,1)S(1)}, bf16[256,2048]{1,0:T(8,128)(2,1)}, u32[]{:S(2)}, u32[]{:S(2)}) collective-permute-start(bf16[256,2048]{1,0:T(8,128)(2,1)S(1)} %bitcast.98), channel_id=1, source_target_pairs={{0,1},{1,2},{2,3},{3,0},{4,5},{5,6},{6,7},{7,4},{8,9},{9,10},{10,1... | collective-permute-start | bytes 3145736 | tf_op jit(solution)/shard_map/ppermute | solution.py:20
  44.5 26.2 %collective-permute-start.6 = (bf16[256,2048]{1,0:T(8,128)(2,1)S(1)}, bf16[256,2048]{1,0:T(8,128)(2,1)}, u32[]{:S(2)}, u32[]{:S(2)}) collective-permute-start(bf16[256,2048]{1,0:T(8,128)(2,1)S(1)} %bitcast.99), channel_id=1, source_target_pairs={{0,3},{1,0},{2,1},{3,2},{4,7},{5,4},{6,5},{7,6},{8,11},{9,8},{10,9... | collective-permute-start | bytes 3145736 | tf_op jit(solution)/shard_map/ppermute | solution.py:20
  48.4 115.3 %all-to-all-start.3 = ((bf16[16,16,2048]{2,1,0:T(8,128)(2,1)}), bf16[16,16,2048]{2,1,0:T(8,128)(2,1)S(1)}, u32[]{:S(2)}, u32[]{:S(2)}) async-start(bf16[16,16,2048]{2,1,0:T(8,128)(2,1)} %gather_fusion.2), calls=%async_computation.3 | async-start | bytes 2097152 | tf_op jit(solution)/shard_map/all_to_all | solution.py:171
  70.7 18.9 %collective-permute-start.3 = (bf16[128,2048]{1,0:T(8,128)(2,1)}, bf16[128,2048]{1,0:T(8,128)(2,1)}, u32[]{:S(2)}, u32[]{:S(2)}) collective-permute-start(bf16[128,2048]{1,0:T(8,128)(2,1)} %slice.33), channel_id=1, source_target_pairs={{0,1},{1,2},{2,3},{3,0},{4,5},{5,6},{6,7},{7,4},{8,9},{9,10},{10,1... | collective-permute-start | bytes 1572872 | tf_op jit(solution)/shard_map/ppermute | solution.py:20
  72.6 21.7 %collective-permute-start.7 = (bf16[128,2048]{1,0:T(8,128)(2,1)}, bf16[128,2048]{1,0:T(8,128)(2,1)S(1)}, u32[]{:S(2)}, u32[]{:S(2)}) collective-permute-start(bf16[128,2048]{1,0:T(8,128)(2,1)} %slice.37), channel_id=1, source_target_pairs={{0,3},{1,0},{2,1},{3,2},{4,7},{5,4},{6,5},{7,6},{8,11},{9,8},{10,9... | collective-permute-start | bytes 1572872 | tf_op jit(solution)/shard_map/ppermute | solution.py:20
  105.3 21.3 %collective-permute-start.4 = (bf16[128,2048]{1,0:T(8,128)(2,1)}, bf16[128,2048]{1,0:T(8,128)(2,1)}, u32[]{:S(2)}, u32[]{:S(2)}) collective-permute-start(bf16[128,2048]{1,0:T(8,128)(2,1)} %fusion.7), channel_id=1, source_target_pairs={{0,3},{1,0},{2,1},{3,2},{4,7},{5,4},{6,5},{7,6},{8,11},{9,8},{10,9... | collective-permute-start | bytes 1572872 | tf_op jit(solution)/shard_map/ppermute | solution.py:20
  111.8 5.9 %copy-start.5 = (bf16[256,2048]{1,0:T(8,128)(2,1)}, bf16[256,2048]{1,0:T(8,128)(2,1)S(1)}, u32[]{:S(2)}) copy-start(bf16[256,2048]{1,0:T(8,128)(2,1)S(1)} %fusion.5) | copy-start | bytes 3145732
  117.7 12.8 %collective-permute-start.8 = (bf16[128,2048]{1,0:T(8,128)(2,1)}, bf16[128,2048]{1,0:T(8,128)(2,1)}, u32[]{:S(2)}, u32[]{:S(2)}) collective-permute-start(bf16[128,2048]{1,0:T(8,128)(2,1)} %fusion.8), channel_id=1, source_target_pairs={{0,1},{1,2},{2,3},{3,0},{4,5},{5,6},{6,7},{7,4},{8,9},{9,10},{10,1... | collective-permute-start | bytes 1572872 | tf_op jit(solution)/shard_map/ppermute | solution.py:20
  119.1 8.9 %slice-start.1 = ((bf16[256,2048]{1,0:T(8,128)(2,1)}), bf16[128,2048]{1,0:T(8,128)(2,1)S(1)}, s32[]{:S(2)}) async-start(bf16[256,2048]{1,0:T(8,128)(2,1)} %copy-done.5), calls=%async_computation.5 | async-start | bytes 1048576 | tf_op jit(solution)/shard_map/slice | solution.py:139
  125.5 1.0 copy-start.3
  126.5 4.0 %copy-start.4 = (bf16[256,2048]{1,0:T(8,128)(2,1)S(1)}, bf16[256,2048]{1,0:T(8,128)(2,1)}, u32[]{:S(2)}) copy-start(bf16[256,2048]{1,0:T(8,128)(2,1)} %copy-done.3) | copy-start | bytes 3145732
  126.5 5.1 %slice-start = ((bf16[256,2048]{1,0:T(8,128)(2,1)}), bf16[128,2048]{1,0:T(8,128)(2,1)S(1)}, s32[]{:S(2)}) async-start(bf16[256,2048]{1,0:T(8,128)(2,1)} %copy-done.3), calls=%async_computation.4 | async-start | bytes 1048576 | tf_op jit(solution)/shard_map/slice | solution.py:142
  129.1 22.6 %collective-permute-start.5 = (bf16[256,2048]{1,0:T(8,128)(2,1)}, bf16[256,2048]{1,0:T(8,128)(2,1)}, u32[]{:S(2)}, u32[]{:S(2)}) collective-permute-start(bf16[256,2048]{1,0:T(8,128)(2,1)} %pad_maximum_fusion), channel_id=1, source_target_pairs={{0,3},{1,0},{2,1},{3,2},{4,7},{5,4},{6,5},{7,6},{8,11},{9,8},{10,9... | collective-permute-start | bytes 3145736 | tf_op jit(solution)/shard_map/ppermute | solution.py:20
  132.8 23.2 %copy-start.7 = (bf16[8,32,2048]{2,1,0:T(8,128)(2,1)S(1)}, bf16[8,32,2048]{2,1,0:T(8,128)(2,1)}, u32[]{:S(2)}) copy-start(bf16[8,32,2048]{2,1,0:T(8,128)(2,1)} %copy-done.6) | copy-start | bytes 3145732
  132.8 23.2 %collective-permute-start.9 = (bf16[256,2048]{1,0:T(8,128)(2,1)}, bf16[256,2048]{1,0:T(8,128)(2,1)}, u32[]{:S(2)}, u32[]{:S(2)}) collective-permute-start(bf16[256,2048]{1,0:T(8,128)(2,1)} %pad_maximum_fusion.1), channel_id=1, source_target_pairs={{0,1},{1,2},{2,3},{3,0},{4,5},{5,6},{6,7},{7,4},{8,9},{9,10},{10,1... | collective-permute-start | bytes 3145736 | tf_op jit(solution)/shard_map/ppermute | solution.py:20
  140.3 27.2 %copy-start.2 = (bf16[1,128,2048]{2,1,0:T(8,128)(2,1)S(1)}, bf16[1,128,2048]{2,1,0:T(8,128)(2,1)}, u32[]{:S(2)}) copy-start(bf16[1,128,2048]{2,1,0:T(8,128)(2,1)} %param.10) | copy-start | bytes 1572868
  163.8 37.4 %copy-start.10 = (s32[8]{0:T(128)S(1)}, s32[8]{0:T(128)}, u32[]{:S(2)}) copy-start(s32[8]{0:T(128)} %param.16) | copy-start | bytes 100
  163.8 38.4 %copy-start.9 = (s32[1,128,2]{1,2,0:T(2,128)S(1)}, s32[1,128,2]{1,2,0:T(2,128)}, u32[]{:S(2)}) copy-start(s32[1,128,2]{1,2,0:T(2,128)} %param.15) | copy-start | bytes 3076
  163.8 39.1 %copy-start.8 = (s32[512]{0:T(512)S(1)}, s32[512]{0:T(512)}, u32[]{:S(2)}) copy-start(s32[512]{0:T(512)} %param.17) | copy-start | bytes 6148
  163.8 29.5 %all-to-all-start.2 = ((bf16[8,32,2048]{2,1,0:T(8,128)(2,1)}), bf16[8,32,2048]{2,1,0:T(8,128)(2,1)S(1)}, u32[]{:S(2)}, u32[]{:S(2)}) async-start(bf16[8,32,2048]{2,1,0:T(8,128)(2,1)} %bitcast.102), calls=%async_computation.2 | async-start | bytes 2097152 | tf_op jit(solution)/shard_map/all_to_all | solution.py:149
  193.3 11.2 %copy-start.1 = (bf16[8,32,2048]{2,1,0:T(8,128)(2,1)}, bf16[8,32,2048]{2,1,0:T(8,128)(2,1)S(1)}, u32[]{:S(2)}) copy-start(bf16[8,32,2048]{2,1,0:T(8,128)(2,1)S(1)} %all-to-all-done.2) | copy-start | bytes 3145732
  193.3 36.1 %all-to-all-start = ((bf16[16,16,2048]{2,1,0:T(8,128)(2,1)}), bf16[16,16,2048]{2,1,0:T(8,128)(2,1)}, u32[]{:S(2)}, u32[]{:S(2)}) async-start(bf16[16,16,2048]{2,1,0:T(8,128)(2,1)} %gather_fusion), calls=%async_computation | async-start | bytes 2097152 | tf_op jit(solution)/shard_map/all_to_all | solution.py:171
  207.6 23.5 %collective-permute-start.10 = (bf16[128,2048]{1,0:T(8,128)(2,1)}, bf16[128,2048]{1,0:T(8,128)(2,1)S(1)}, u32[]{:S(2)}, u32[]{:S(2)}) collective-permute-start(bf16[128,2048]{1,0:T(8,128)(2,1)} %get-tuple-element.8), channel_id=1, source_target_pairs={{0,64},{64,128},{128,192},{1,65},{65,129},{129,193},{2,66},{66,130... | collective-permute-start | bytes 1572872 | tf_op jit(solution)/shard_map/ppermute | solution.py:182
